TPU v7x, 64 devices: a 2x2x8 block of a 4x4x8 slice. The times are simulated.
64 devices in a mesh: dp: 4 (over x, y), ep: 16 (over z, core).
Axes of the slice: x: 2, y: 2, z: 8, core: 2. Of those that a mesh axis runs over, the one named last changes fastest.
The devices are a block of a 4x4x8 slice.
Arguments:
- x_tokens: bfloat16 [4096, 2048], P(('dp', 'ep')), parts along dimension 0
- slot_expert: int32 [80], replicated
- w1_slots: bfloat16 [80, 2048, 1408], P('ep')
- w3_slots: bfloat16 [80, 2048, 1408], P('ep')
- w2_slots: bfloat16 [80, 1408, 2048], P('ep')
- assign: int32 [4096, 6], P(('dp', 'ep')), parts along dimension 0
- w_router: bfloat16 [2048, 64], replicated
- w1_shared: bfloat16 [2048, 2816], replicated
- w3_shared: bfloat16 [2048, 2816], replicated
- w2_shared: bfloat16 [2816, 2048], replicated
Outputs:
- output: bfloat16 [4096, 2048], P(('dp', 'ep')), parts along dimension 0
There are 4 independent parts. A program takes and returns all parts, laid end to end along the dimension named above; an argument that names none is the same for every part.
All inputs are finite; a program needn't handle non-finite values.
Results may differ from a plain program's by a relative error of at most 0.00157.
Values are sent between devices in bfloat16 or wider.
A program may use at most 768 MiB of HBM per device.

v0:
```python
import jax
import jax.numpy as jnp
from jax import lax
from jax.sharding import PartitionSpec as P

ROUTE_SCALE = 2.5


def gate_weights(x_tokens, assign, slot_expert, w_router):
    logits = jnp.dot(x_tokens, w_router, preferred_element_type=jnp.float32)
    gate_prob = jax.nn.sigmoid(logits)
    is_kept = assign >= 0
    chosen = jnp.take(slot_expert, jnp.maximum(assign, 0))
    picked = jnp.where(is_kept, jnp.take_along_axis(gate_prob, chosen, axis=1), 0.0)
    gate_total = jnp.sum(picked, axis=1, keepdims=True)
    return ROUTE_SCALE * picked / jnp.maximum(gate_total, 1e-30), is_kept


def shared_expert(x_tokens, w1_shared, w3_shared, w2_shared):
    h_gate = jnp.dot(x_tokens, w1_shared, preferred_element_type=jnp.float32)
    h_up = jnp.dot(x_tokens, w3_shared, preferred_element_type=jnp.float32)
    mid_act = (jax.nn.silu(h_gate) * h_up).astype(jnp.bfloat16)
    return jnp.dot(mid_act, w2_shared, preferred_element_type=jnp.float32)


def solution(mesh):
    group_size = mesh.shape['ep']

    def device_step(x_tokens, slot_expert, w1_slots, w3_slots, w2_slots, assign, w_router, w1_shared, w3_shared, w2_shared):
        tok_dev, dim_model = x_tokens.shape
        top_k = assign.shape[1]
        local_slots = w1_slots.shape[0]
        num_slots = local_slots * group_size
        cap_rows = max(4, (3 * tok_dev * top_k) // num_slots)
        route_weight, is_kept = gate_weights(x_tokens, assign, slot_expert, w_router)
        shared_out = shared_expert(x_tokens, w1_shared, w3_shared, w2_shared)
        flat_slot = jnp.where(is_kept, assign, num_slots).reshape(-1)
        onehot = (flat_slot[:, None] == jnp.arange(num_slots, dtype=jnp.int32)[None, :]).astype(jnp.int32)
        slot_rank = jnp.sum(jnp.cumsum(onehot, axis=0) * onehot, axis=1) - 1
        dummy_row = num_slots * cap_rows
        row_pos = jnp.where(flat_slot < num_slots, flat_slot * cap_rows + slot_rank, dummy_row)
        token_ids = jnp.arange(tok_dev * top_k, dtype=jnp.int32) // top_k
        row_token = jnp.full((dummy_row + 1,), tok_dev, jnp.int32).at[row_pos].set(token_ids)[:dummy_row]
        send_rows = jnp.take(x_tokens, row_token, axis=0, mode='fill', fill_value=0)
        recv_rows = lax.all_to_all(send_rows, 'ep', 0, 0, tiled=True)
        recv_rows = recv_rows.reshape(group_size, local_slots, cap_rows, dim_model)
        h_gate = jnp.einsum('jlcd,ldf->jlcf', recv_rows, w1_slots, preferred_element_type=jnp.float32)
        h_up = jnp.einsum('jlcd,ldf->jlcf', recv_rows, w3_slots, preferred_element_type=jnp.float32)
        mid_act = (jax.nn.silu(h_gate) * h_up).astype(jnp.bfloat16)
        expert_out = jnp.einsum('jlcf,lfd->jlcd', mid_act, w2_slots, preferred_element_type=jnp.float32).astype(jnp.bfloat16)
        back_rows = lax.all_to_all(expert_out.reshape(dummy_row, dim_model), 'ep', 0, 0, tiled=True)
        gathered = jnp.take(back_rows, jnp.minimum(row_pos, dummy_row - 1), axis=0).reshape(tok_dev, top_k, dim_model)
        routed = jnp.sum(route_weight[:, :, None] * gathered, axis=1)
        return (shared_out + routed).astype(jnp.bfloat16)

    token_spec = P(('dp', 'ep'), None)
    slot_spec = P('ep', None, None)
    return jax.shard_map(device_step, mesh=mesh, in_specs=(token_spec, P(), slot_spec, slot_spec, slot_spec, token_spec, P(), P(), P(), P()), out_specs=token_spec, check_vma=False)
```

profile of v0, /device:TPU:21, one launch (start us, length us, event | category | flops | bytes accessed | tf_op | source)
XLA Modules:
  0.0 339.1 jit_solution(17251967513816698667)
XLA Ops:
  0.0 0.8 copy.15
  1.1 0.9 reduce-window.6
  2.1 0.2 slice_reduce_fusion
  3.0 2.9 scatter_custom_fusion
  6.0 6.0 %gather_fusion.1 = bf16[1120,2048]{1,0:T(8,128)(2,1)} fusion(bf16[64,2048]{1,0:T(8,128)(2,1)S(1)} %copy-done, s32[2048]{0:T(1024)S(1)} %pad_clamp_fusion), kind=kCustom, calls=%fused_computation.1 | custom fusion | bytes 9179520 | tf_op jit(solution)/shard_map/jit(_take)/gather | solution.py:44
  11.9 5.4 %gather.23 = bf16[16,70,2048]{2,1,0:T(8,128)(2,1)} reshape(bf16[1120,2048]{1,0:T(8,128)(2,1)} %gather_fusion.1) | data formatting | bytes 9175040 | tf_op jit(solution)/shard_map/jit(_take)/gather | solution.py:44
  17.4 2.7 broadcast_select_fusion
  20.1 117.5 %all_to_all.18 = bf16[16,70,2048]{2,1,0:T(8,128)(2,1)S(1)} all-to-all(bf16[16,70,2048]{2,1,0:T(8,128)(2,1)S(1)} %broadcast_select_fusion), channel_id=1, replica_groups=mesh['dp'=4,'ep'=16] {'ep'}, dimensions={0} | all-to-all | bytes 9175040 | tf_op jit(solution)/shard_map/all_to_all | solution.py:45
  137.6 4.7 %copy.19 = bf16[16,70,2048]{2,0,1:T(8,128)(2,1)} copy(bf16[16,70,2048]{2,1,0:T(8,128)(2,1)S(1)} %all_to_all.18) | data formatting | bytes 9175040 | tf_op jit(solution)/shard_map/all_to_all | solution.py:45
  142.3 15.9 %fusion.2 = f32[5,16,14,1408]{3,1,2,0:T(8,128)} fusion(bf16[16,5,14,2048]{3,0,2,1:T(8,128)(2,1)} %bitcast.70, bf16[5,2048,1408]{2,1,0:T(8,128)(2,1)} %param.13), kind=kOutput, calls=%fused_computation.7 | convolution fusion | flops 6459228160 | bytes 39731200 | tf_op jit(solution)/shard_map/jlcd,ldf->jlcf/dot_general | solution.py:48
  158.2 21.2 %fusion.6 = bf16[16,5,14,1408]{3,0,2,1:T(8,128)(2,1)} fusion(f32[5,16,14,1408]{3,1,2,0:T(8,128)} %fusion.2, bf16[16,5,14,2048]{3,0,2,1:T(8,128)(2,1)} %bitcast.71, bf16[5,2048,1408]{2,1,0:T(8,128)(2,1)} %param.12), kind=kOutput, calls=%fused_computation.12 | convolution fusion | flops 6468689920 | bytes 42885120 | tf_op jit(solution)/shard_map/jlcd,ldf->jlcf/dot_general | solution.py:47
  179.4 13.9 %fusion.12 = bf16[5,16,14,2048]{3,1,2,0:T(8,128)(2,1)S(1)} fusion(bf16[16,5,14,1408]{3,0,2,1:T(8,128)(2,1)} %fusion.6, bf16[5,1408,2048]{2,1,0:T(8,128)(2,1)} %param.14), kind=kOutput, calls=%fused_computation.20 | convolution fusion | flops 6461521920 | bytes 36577280 | tf_op jit(solution)/shard_map/jlcf,lfd->jlcd/dot_general | solution.py:50
  193.3 4.7 %copy.20 = bf16[16,70,2048]{2,1,0:T(8,128)(2,1)} copy(bf16[16,70,2048]{2,0,1:T(8,128)(2,1)S(1)} %bitcast.72) | data formatting | bytes 9175040 | tf_op jit(solution)/shard_map/all_to_all | solution.py:51
  198.0 5.1 %all-to-all-start.1 = ((bf16[16,70,2048]{2,1,0:T(8,128)(2,1)}), bf16[16,70,2048]{2,1,0:T(8,128)(2,1)}, u32[]{:S(2)}, u32[]{:S(2)}) async-start(bf16[16,70,2048]{2,1,0:T(8,128)(2,1)} %copy.20), calls=%async_computation.1 | async-start | bytes 9437184 | tf_op jit(solution)/shard_map/all_to_all | solution.py:51
  203.2 2.7 gather_fusion
  206.3 0.2 fusion.19
  206.5 2.9 gather_fusion.3
  209.8 6.4 %fusion.34 = f32[64,2816]{1,0:T(8,128)S(1)} fusion(bf16[64,2048]{1,0:T(8,128)(2,1)S(1)} %copy-done, bf16[2048,2816]{1,0:T(8,128)(2,1)} %param.17), kind=kOutput, calls=%fused_computation.73 | convolution fusion | flops 738197504 | bytes 12517376 | tf_op jit(solution)/shard_map/dot_general | solution.py:20
  216.1 91.3 %all-to-all-done.1 = bf16[16,70,2048]{2,1,0:T(8,128)(2,1)} async-done(((bf16[16,70,2048]{2,1,0:T(8,128)(2,1)}), bf16[16,70,2048]{2,1,0:T(8,128)(2,1)}, u32[]{:S(2)}, u32[]{:S(2)}) %all-to-all-start.1) | async-done | bytes 4587552 | tf_op jit(solution)/shard_map/all_to_all | solution.py:51
  307.4 5.5 %all_to_all.15 = bf16[1120,2048]{1,0:T(8,128)(2,1)} reshape(bf16[16,70,2048]{2,1,0:T(8,128)(2,1)} %all-to-all-done.1) | data formatting | bytes 9175040 | tf_op jit(solution)/shard_map/all_to_all | solution.py:51
  312.9 8.0 %gather_fusion.2 = bf16[384,2048]{1,0:T(8,128)(2,1)} fusion(bf16[1120,2048]{1,0:T(8,128)(2,1)} %all_to_all.15, s32[1024]{0:T(1024)S(1)} %pad_clamp_fusion.1), kind=kCustom, calls=%fused_computation.2 | custom fusion | bytes 3147264 | tf_op jit(solution)/shard_map/jit(_take)/gather | solution.py:52
  320.8 2.5 gather.25
  323.3 3.3 multiply_reduce_fusion
  326.6 12.5 %fusion.16 = bf16[64,2048]{1,0:T(8,128)(2,1)} fusion(f32[64,2048]{1,0:T(8,128)} %multiply_reduce_fusion, bf16[2816,2048]{1,0:T(8,128)(2,1)} %param.19, bf16[64,2048]{1,0:T(8,128)(2,1)S(1)} %copy-done, bf16[2048,2816]{1,0:T(8,128)(2,1)} %param.18, f32[64,2816]{1,0:T(8,128)S(1)} %fusion.34), kind=kOutput, calls=%fused_computation.24 | convolution fusion | flops 1477738496 | bytes 24838144 | tf_op jit(solution)/shard_map/dot_general | solution.py:23
  (33 shorter events, 1.8 us)
Async XLA Ops:
  0.0 6.0 %copy-start = (bf16[64,2048]{1,0:T(8,128)(2,1)S(1)}, bf16[64,2048]{1,0:T(8,128)(2,1)}, u32[]{:S(2)}) copy-start(bf16[64,2048]{1,0:T(8,128)(2,1)} %param.10) | copy-start | bytes 786436
  198.0 5.2 %copy-start.1 = (s32[80]{0:T(128)S(1)}, s32[80]{0:T(128)}, u32[]{:S(2)}) copy-start(s32[80]{0:T(128)} %param.11) | copy-start | bytes 964
  198.0 109.4 %all-to-all-start.1 = ((bf16[16,70,2048]{2,1,0:T(8,128)(2,1)}), bf16[16,70,2048]{2,1,0:T(8,128)(2,1)}, u32[]{:S(2)}, u32[]{:S(2)}) async-start(bf16[16,70,2048]{2,1,0:T(8,128)(2,1)} %copy.20), calls=%async_computation.1 | async-start | bytes 9437184 | tf_op jit(solution)/shard_map/all_to_all | solution.py:51
  203.2 3.0 copy-start.2
where the time goes:
time: 340 us; the launch traced here: 339 us
  blocking collectives  118 us (35%)
  waiting for transfers between devices  91.3 us (27%)
  matrix products  70 us (21%)
  local copies, waits for them, and re-layouts  47.5 us (14%)
  other arithmetic  7.52 us (2%)
  starting transfers between devices  5.06 us (1%)
    all_to_all x1, blocking collectives, device_step(): recv_rows = lax.all_to_all(send_rows, 'ep', 0, 0, tiled=True)  118 us
    all_to_all x1, waiting for transfers between devices, device_step(): lax.all_to_all(expert_out.reshape(dummy_row, dim_model), 'ep', 0, 0, tile...  91.3 us
    dot_general x1, matrix products, device_step(): jnp.einsum('jlcd,ldf->jlcf', recv_rows, w1_slots, preferred_element_type=...  21.2 us
    dot_general x1, matrix products, device_step(): jnp.einsum('jlcd,ldf->jlcf', recv_rows, w3_slots, preferred_element_type=...  15.9 us
    dot_general x1, matrix products, device_step(): jnp.einsum('jlcf,lfd->jlcd', mid_act, w2_slots, preferred_element_type=jn...  13.9 us
    dot_general x1, matrix products, shared_expert(): return jnp.dot(mid_act, w2_shared, preferred_element_type=jnp.float32)  12.5 us
    gather x2, local copies, waits for them, and re-layouts, device_step(): send_rows = jnp.take(x_tokens, row_token, axis=0, mode='fill', fill_value=0)  11.3 us
    gather x2, local copies, waits for them, and re-layouts, device_step(): jnp.take(back_rows, jnp.minimum(row_pos, dummy_row - 1), axis=0)  10.4 us
  transfers between devices with their start and end apart: 1, of which 1 were waited for; matrix products, arithmetic and copies ran while one was open for 4% of the time, Pallas kernels for 0%

commit v1 on v0

v1 whole, which is shorter than its diff:
```python
import functools

import jax
import jax.numpy as jnp
from jax import lax
from jax.experimental import pallas as pl
from jax.experimental.pallas import tpu as pltpu
from jax.sharding import PartitionSpec as P

ROUTE_SCALE = 2.5
MESH = pl.DeviceIdType.MESH
LANES = 128
CAP = 16
A_RING = 3
B_RING = 6
COL_CHUNKS = 4

F32 = jnp.float32
BF16 = jnp.bfloat16


def kernel(
    group, x_ref, asg_ref, se_ref, wr_ref, w1, w3, w2, v1, v3, v2, y_ref,
    xall, tall, tsend, xg, h, ob, osib, s1, r1, sn, rn, zsh, hs, wcs, abuf, bbuf,
    xs_sem, xr_sem, xds_sem, xdr_sem, ts_sem, tr_sem, tds_sem, tdr_sem,
    os_sem, or_sem, rs_sem, rr_sem, a_sem, b_sem,
):
    tok, dim = x_ref.shape
    top_k = asg_ref.shape[1]
    slots, _, ff = w1.shape
    ff_sh = v1.shape[1]
    nz = group // 2
    half_tok = tok // 2
    nc = COL_CHUNKS
    cw = dim // nc
    hw = cw // 2
    wide = -(-(ff // LANES) // 2) * LANES
    widths = (wide, ff - wide)
    sh_units = [(o, min(wide, ff_sh - o)) for o in range(0, ff_sh, wide)]
    nsu = len(sh_units)
    sh_pieces = ff_sh // ff

    me = lax.axis_index("ep")
    z = me // 2
    c = me % 2
    sib = 2 * z + (1 - c)

    def at(zz):
        return lax.rem(zz + 2 * nz, nz)

    nb = (2 * at(z + 1) + c, 2 * at(z - 1) + c)

    def remote(src, dst, ssem, rsem, dev):
        return pltpu.make_async_remote_copy(
            src_ref=src, dst_ref=dst, send_sem=ssem, recv_sem=rsem, device_id={"ep": dev}, device_id_type=MESH
        )

    def away(d, s):
        return at(z - s) if d == 0 else at(z + s)

    def a_copies(u_slot, first, second, width):
        return [
            pltpu.make_async_copy(src, abuf.at[u_slot, i, :, pl.ds(0, width)], a_sem.at[u_slot, i])
            for i, src in enumerate((first, second))
        ]

    def a_shared(u):
        off, width = sh_units[u]
        cols = pl.ds(off, width)
        return a_copies(u % A_RING, v1.at[:, cols], v3.at[:, cols], width)

    def a_routed(l, half):
        cols = pl.ds(half * wide, widths[half])
        slot = lax.rem(nsu + 2 * l + half, A_RING)
        return a_copies(slot, w1.at[l, :, cols], w3.at[l, :, cols], widths[half])

    def a_start(u):
        for cp in a_shared(u) if u < nsu else a_routed((u - nsu) // 2, (u - nsu) % 2):
            cp.start()

    nsb = sh_pieces * nc

    def b_shared(v):
        q, p = v // sh_pieces, v % sh_pieces
        return pltpu.make_async_copy(v2.at[pl.ds(p * ff, ff), pl.ds(q * cw, cw)], bbuf.at[v % B_RING], b_sem.at[v % B_RING])

    def b_routed(i):
        q, l = i // slots, i % slots
        slot = (nsb + i) % B_RING
        return pltpu.make_async_copy(w2.at[l, :, pl.ds(pl.multiple_of(q * cw, LANES), cw)], bbuf.at[slot], b_sem.at[slot])

    def b_start(v):
        (b_shared(v) if v < nsb else b_routed(v - nsb)).start()

    for u in range(A_RING):
        a_start(u)
    for v in range(B_RING):
        b_start(v)

    barrier = pltpu.get_barrier_semaphore()
    for peer in (nb[0], nb[1], sib):
        pl.semaphore_signal(barrier, inc=1, device_id={"ep": peer}, device_id_type=MESH)
    pl.semaphore_wait(barrier, 3)

    def x_part(d, m):
        return m // 2 + 1, pl.ds(((m % 2) ^ d) * half_tok, half_tok)

    def x_send(d, m):
        s, rows = x_part(d, m)
        blk = 2 * away(d, s - 1) + c
        src = x_ref.at[rows] if s == 1 else xall.at[blk, rows]
        return remote(src, xall.at[blk, rows], xs_sem.at[d, m], xr_sem.at[d, m], nb[d])

    def x_recv(d, m):
        s, rows = x_part(d, m)
        blk = 2 * away(d, s) + c
        return remote(xall.at[blk, rows], xall.at[blk, rows], xs_sem.at[d, m], xr_sem.at[d, m], nb[d])

    def x_cross(d, m, core):
        s, rows = x_part(d, m)
        blk = 2 * away(d, s) + core
        return remote(xall.at[blk, rows], xall.at[blk, rows], xds_sem.at[d * 7 + m], xdr_sem.at[d * 7 + m], sib)

    def x_cross_own(blk):
        return remote(x_ref, xall.at[blk], xds_sem.at[14], xdr_sem.at[14], sib)

    def t_send(d, m):
        blk = 2 * away(d, m) + c
        src = tsend if m == 0 else tall.at[blk]
        return remote(src, tall.at[blk], ts_sem.at[d, m], tr_sem.at[d, m], nb[d])

    def t_recv(d, m):
        blk = 2 * away(d, m + 1) + c
        return remote(tall.at[blk], tall.at[blk], ts_sem.at[d, m], tr_sem.at[d, m], nb[d])

    def t_cross(d, m, core):
        blk = 2 * away(d, m + 1) + core
        return remote(tall.at[blk], tall.at[blk], tds_sem.at[d * 4 + m], tdr_sem.at[d * 4 + m], sib)

    def t_cross_own(blk):
        return remote(tsend, tall.at[blk], tds_sem.at[7], tdr_sem.at[7], sib)

    t_last = (3, 2)

    def take_x(m):
        for d in (0, 1):
            x_recv(d, m).wait_recv()
            if m + 2 <= 6:
                x_send(d, m + 2).start()
            x_cross(d, m, c).start()

    def take_t(m):
        for d in (0, 1):
            if m <= t_last[d]:
                t_recv(d, m).wait_recv()
                if m + 1 <= t_last[d]:
                    t_send(d, m + 1).start()
                t_cross(d, m, c).start()

    for m in (0, 1):
        for d in (0, 1):
            x_send(d, m).start()
    x_cross_own(me).start()

    num_slots = se_ref.shape[1]
    num_exp = wr_ref.shape[1]
    exp_ids = lax.broadcasted_iota(jnp.int32, (num_exp, LANES), 0)
    slot_lane = jnp.concatenate([se_ref[...], jnp.full((1, LANES - num_slots), -1, jnp.int32)], axis=1)
    holds = jnp.where(exp_ids == slot_lane, 1.0, 0.0).astype(BF16)
    w_slot = jnp.dot(wr_ref[...], holds, preferred_element_type=F32).astype(BF16)
    gate = jax.nn.sigmoid(jnp.dot(x_ref[...], w_slot, preferred_element_type=F32))
    lane = lax.broadcasted_iota(jnp.int32, (tok, LANES), 1)
    asg = asg_ref[...]
    picked = [
        jnp.sum(jnp.where(lane == asg[:, k : k + 1], gate, 0.0), axis=1, keepdims=True) for k in range(top_k)
    ]
    total = functools.reduce(lambda a, b: a + b, picked)
    table = jnp.full((tok, LANES), -1.0, F32)
    for k in range(top_k):
        table = jnp.where(lane == k, asg[:, k : k + 1].astype(F32), table)
        table = jnp.where(lane == 8 + k, ROUTE_SCALE * picked[k] / jnp.maximum(total, 1e-30), table)
    table = jnp.concatenate([table, jnp.full((LANES - tok, LANES), -1.0, F32)], axis=0)
    table = jnp.transpose(table)[:16]
    tsend[...] = table
    tall[me] = table
    xall[me] = x_ref[...]

    def shared_up(u):
        for cp in a_shared(u):
            cp.wait()
        off, width = sh_units[u]
        slot = u % A_RING
        up = jnp.dot(x_ref[...], abuf[slot, 0, :, :width], preferred_element_type=F32)
        lin = jnp.dot(x_ref[...], abuf[slot, 1, :, :width], preferred_element_type=F32)
        hs[:, off : off + width] = (jax.nn.silu(up) * lin).astype(BF16)
        if u + A_RING < nsu + 2 * slots:
            a_start(u + A_RING)

    def shared_down(q):
        acc = None
        for p in range(sh_pieces):
            v = q * sh_pieces + p
            b_shared(v).wait()
            part = jnp.dot(hs[:, p * ff : (p + 1) * ff], bbuf[v % B_RING], preferred_element_type=F32)
            acc = part if acc is None else acc + part
            b_start(v + B_RING)
        zsh[:, q * cw : (q + 1) * cw] = acc

    tri = jnp.where(
        lax.broadcasted_iota(jnp.int32, (LANES, LANES), 0) < lax.broadcasted_iota(jnp.int32, (LANES, LANES), 1), 1.0, 0.0
    ).astype(BF16)
    seg = slots * CAP

    def choose(tab, rows, slot_of):
        row = lax.broadcasted_iota(jnp.int32, (rows, LANES), 0)
        want = slot_of(row // CAP).astype(F32)
        named = jnp.zeros((rows, LANES), F32)
        weight = jnp.zeros((rows, LANES), F32)
        for k in range(top_k):
            hit = tab[k : k + 1, :] == want
            named = jnp.where(hit, 1.0, named)
            weight = jnp.where(hit, tab[8 + k : 9 + k, :], weight)
        rank = jnp.dot(named.astype(BF16), tri, preferred_element_type=F32)
        return (named > 0.0) & (rank == (row % CAP).astype(F32)), weight

    def dispatch(zz):
        def one(core, _):
            j = 2 * zz + core
            mine, _w = choose(tall[j], seg, lambda i: me * slots + i)
            pick = jnp.where(mine, 1.0, 0.0).astype(BF16)[:, :tok]
            rows = jnp.dot(pick, xall[j], preferred_element_type=F32).astype(BF16)
            for l in range(slots):
                xg[l, core * nz + zz] = rows[l * CAP : (l + 1) * CAP]
            return 0

        lax.fori_loop(0, 2, one, 0)

    def weigh(zz):
        mine, weight = choose(
            tall[2 * zz + c], 2 * seg, lambda i: jnp.where(i < slots, me * slots + i, sib * slots + i - slots)
        )
        full = jnp.where(mine, weight, 0.0)
        full = jnp.concatenate([full, jnp.zeros((2 * LANES - 2 * seg, LANES), F32)], axis=0)
        full = jnp.transpose(full)[:tok]
        hi = full.astype(BF16)
        rest = full - hi.astype(F32)
        mid = rest.astype(BF16)
        low = (rest - mid.astype(F32)).astype(BF16)
        wcs[zz] = jnp.concatenate([hi, mid, low], axis=0)

    def ready(s):
        if s == 0:
            x_cross_own(sib).wait_recv()
            t_cross_own(sib).wait_recv()
            spots = (z,)
        elif s < nz // 2:
            for d in (0, 1):
                x_cross(d, 2 * s - 2, 1 - c).wait_recv()
                x_cross(d, 2 * s - 1, 1 - c).wait_recv()
                t_cross(d, s - 1, 1 - c).wait_recv()
            spots = (away(0, s), away(1, s))
        else:
            for d in (0, 1):
                x_cross(d, 2 * s - 2, 1 - c).wait_recv()
            t_cross(0, s - 1, 1 - c).wait_recv()
            spots = (away(0, s),)
        for zz in spots:
            dispatch(zz)
            weigh(zz)

    shared_up(0)
    for d in (0, 1):
        t_send(d, 0).start()
    t_cross_own(me).start()
    take_x(0)
    shared_up(1)
    take_x(1)
    take_t(0)
    shared_up(2)
    take_x(2)
    for u in range(3, nsu):
        shared_up(u)
    ready(0)
    take_x(3)
    take_t(1)
    shared_down(0)
    shared_down(1)
    ready(1)
    take_x(4)
    shared_down(2)
    shared_down(3)
    take_x(5)
    take_t(2)
    ready(2)
    take_x(6)
    take_t(3)
    ready(3)
    ready(4)

    def up_slot(l, _):
        rows = xg[l].reshape(group * CAP, dim)
        for half in (0, 1):
            for cp in a_routed(l, half):
                cp.wait()
            slot = lax.rem(nsu + 2 * l + half, A_RING)
            width = widths[half]
            both = jnp.concatenate([abuf[slot, 0, :, :width], abuf[slot, 1, :, :width]], axis=1)
            res = jnp.dot(rows, both, preferred_element_type=F32)
            h[l, :, half * wide : half * wide + width] = (jax.nn.silu(res[:, :width]) * res[:, width:]).astype(BF16)
            ahead = nsu + half + A_RING - nsu
            step, nxt = ahead // 2, ahead % 2

            @pl.when(l + step < slots)
            def _():
                for cp in a_routed(l + step, nxt):
                    cp.start()

        return 0

    lax.fori_loop(0, slots, up_slot, 0)

    def down(q):
        def one(l, _):
            i = q * slots + l
            b_routed(i).wait()
            res = jnp.dot(h[l], bbuf[(nsb + i) % B_RING], preferred_element_type=F32).astype(BF16)
            for core in (0, 1):
                ob[q, core, l] = res[core * nz * CAP : (core + 1) * nz * CAP].reshape(nz, CAP, cw)

            @pl.when(i + B_RING < slots * nc)
            def _():
                b_routed(i + B_RING).start()

            return 0

        lax.fori_loop(0, slots, one, 0)
        o_cross(q).start()

    def o_cross(q):
        return remote(ob.at[q, 1 - c], osib.at[q], os_sem.at[q], or_sem.at[q], sib)

    def partial(zz, q):
        rhs = jnp.concatenate([ob[q, c, :, zz].reshape(seg, cw), osib[q, :, zz].reshape(seg, cw)], axis=0)
        res = jnp.dot(wcs[zz][:, : 2 * seg], rhs, preferred_element_type=F32)
        return res[:tok] + res[tok : 2 * tok] + res[2 * tok :]

    def r_copy(d, q, s):
        src, dst = (s1.at[d, q], r1.at[d, q]) if s == 1 else (sn.at[d, q, s - 2], rn.at[d, q, s - 2])
        return remote(src, dst, rs_sem.at[d, q, s - 1], rr_sem.at[d, q, s - 1], nb[d])

    def sums(q, s):
        if s == 1:
            o_cross(q).wait_recv()
            part = partial(at(z + nz // 2), q)
            s1[0, q] = part[:, :hw]
            s1[1, q] = part[:, hw:]
        else:
            for d in (0, 1):
                part = partial(away(1 - d, nz // 2 + 1 - s), q)
                r_copy(d, q, s - 1).wait_recv()
                if s == 2:
                    lo, hi = part[:, :hw], part[:, hw:]
                    if d == 0:
                        lo = lo + r1[0, q]
                    else:
                        hi = hi + r1[1, q]
                    sn[d, q, 0, :, :hw] = lo
                    sn[d, q, 0, :, hw:] = hi
                else:
                    sn[d, q, s - 2] = part + rn[d, q, s - 3]
        for d in (0, 1):
            r_copy(d, q, s).start()

    def finish(q):
        part = partial(z, q) + zsh[:, q * cw : (q + 1) * cw]
        for d in (0, 1):
            r_copy(d, q, 4).wait_recv()
        y_ref[:, q * cw : (q + 1) * cw] = (part + rn[0, q, 2] + rn[1, q, 2]).astype(y_ref.dtype)

    down(0)
    down(1)
    sums(0, 1)
    down(2)
    sums(0, 2)
    sums(1, 1)
    down(3)
    sums(2, 1)
    sums(1, 2)
    sums(3, 1)
    sums(0, 3)
    sums(2, 2)
    sums(1, 3)
    sums(3, 2)
    sums(2, 3)
    sums(0, 4)
    sums(3, 3)
    sums(1, 4)
    sums(2, 4)
    sums(3, 4)
    for q in range(nc):
        finish(q)

    for d in (0, 1):
        for m in range(7):
            x_send(d, m).wait_send()
            x_cross(d, m, c).wait_send()
        for m in range(t_last[d] + 1):
            t_send(d, m).wait_send()
            t_cross(d, m, c).wait_send()
        for q in range(nc):
            for s in (1, 2, 3, 4):
                r_copy(d, q, s).wait_send()
    x_cross_own(me).wait_send()
    t_cross_own(me).wait_send()
    for q in range(nc):
        o_cross(q).wait_send()


def solution(mesh):
    group = mesh.shape["ep"]

    def device_step(x, slot_expert, w1, w3, w2, assign, w_router, v1, v3, v2):
        tok, dim = x.shape
        slots, _, ff = w1.shape
        nz = group // 2
        nc = COL_CHUNKS
        cw = dim // nc
        wide = -(-(ff // LANES) // 2) * LANES
        vmem = pl.BlockSpec(memory_space=pltpu.VMEM)
        hbm = pl.BlockSpec(memory_space=pl.ANY)
        dma = pltpu.SemaphoreType.DMA
        return pl.pallas_call(
            functools.partial(kernel, group),
            out_shape=jax.ShapeDtypeStruct((tok, dim), BF16),
            in_specs=[vmem] * 4 + [hbm] * 6,
            out_specs=vmem,
            scratch_shapes=[
                pltpu.VMEM((group, tok, dim), BF16),
                pltpu.VMEM((group, 16, LANES), F32),
                pltpu.VMEM((16, LANES), F32),
                pltpu.VMEM((slots, group, CAP, dim), BF16),
                pltpu.VMEM((slots, group * CAP, ff), BF16),
                pltpu.VMEM((nc, 2, slots, nz, CAP, cw), BF16),
                pltpu.VMEM((nc, slots, nz, CAP, cw), BF16),
                pltpu.VMEM((2, nc, tok, cw // 2), F32),
                pltpu.VMEM((2, nc, tok, cw // 2), F32),
                pltpu.VMEM((2, nc, 3, tok, cw), F32),
                pltpu.VMEM((2, nc, 3, tok, cw), F32),
                pltpu.VMEM((tok, dim), F32),
                pltpu.VMEM((tok, v1.shape[1]), BF16),
                pltpu.VMEM((nz, 3 * tok, 2 * LANES), BF16),
                pltpu.VMEM((A_RING, 2, dim, wide), BF16),
                pltpu.VMEM((B_RING, ff, cw), BF16),
                dma((2, 7)), dma((2, 7)), dma((15,)), dma((15,)),
                dma((2, 4)), dma((2, 4)), dma((8,)), dma((8,)),
                dma((nc,)), dma((nc,)), dma((2, nc, 4)), dma((2, nc, 4)),
                dma((A_RING, 2)), dma((B_RING,)),
            ],
            compiler_params=pltpu.CompilerParams(
                collective_id=0, has_side_effects=True, vmem_limit_bytes=66 * 1000 * 1000
            ),
            name="moe_step",
        )(x, assign, slot_expert.reshape(1, -1), w_router, w1, w3, w2, v1, v3, v2)

    token_spec = P(("dp", "ep"), None)
    slot_spec = P("ep", None, None)
    return jax.shard_map(
        device_step,
        mesh=mesh,
        in_specs=(token_spec, P(), slot_spec, slot_spec, slot_spec, token_spec, P(), P(), P(), P()),
        out_specs=token_spec,
        check_vma=False,
    )
```

time: 340 us -> 112 us (0.33)
  blocking collectives: 118 us -> 0 us
  Pallas kernels: 0 us -> 105 us
  waiting for transfers between devices: 91.3 us -> 0 us
  matrix products: 70 us -> 0 us
  local copies, waits for them, and re-layouts: 47.5 us -> 5.01 us
  other arithmetic: 7.52 us -> 0 us
  starting transfers between devices: 5.06 us -> 0 us
    all_to_all x1 -> x0, blocking collectives: 118 us -> none  [device_step(): recv_rows = lax.all_to_all(send_rows, 'ep', 0, 0, tiled=True)]
    pallas_call x0 -> x1, Pallas kernels: none -> 105 us  [device_step(): pl.pallas_call(functools.partial(kernel, group), out_shape=jax.ShapeDtype...]
    all_to_all x1 -> x0, waiting for transfers between devices: 91.3 us -> none  [device_step(): lax.all_to_all(expert_out.reshape(dummy_row, dim_model), 'ep', 0, 0, tile...]
    dot_general x6 -> x0, matrix products: 70 us -> none  [the longest x1 21.2 us: device_step(): jnp.einsum('jlcd,ldf->jlcf', recv_rows, w1_slots, preferred_element_type=...]
    gather x9 -> x0, local copies, waits for them, and re-layouts: 27.7 us -> none  [the longest x2 11.3 us: device_step(): send_rows = jnp.take(x_tokens, row_token, axis=0, mode='fill', fill_value=0)]
    all_to_all x3 -> x0, local copies, waits for them, and re-layouts: 14.8 us -> none  [the longest x2 10.1 us: device_step(): lax.all_to_all(expert_out.reshape(dummy_row, dim_model), 'ep', 0, 0, tile...]
    all_to_all x1 -> x0, starting transfers between devices: 5.06 us -> none  [device_step(): lax.all_to_all(expert_out.reshape(dummy_row, dim_model), 'ep', 0, 0, tile...]
    unnamed x7 -> x3, local copies, waits for them, and re-layouts: 0.83 us -> 5.01 us
  transfers between devices with their start and end apart: 1 -> 0, of which waited for: 1 -> 0; matrix products, arithmetic and copies ran while one was open for 4% -> 0% of each run, Pallas kernels for 0% -> 0%
where the time goes in v1:
time: 112 us; the launch traced here: 110 us
  Pallas kernels  105 us (94%)
  local copies, waits for them, and re-layouts  5.01 us (4%)
    pallas_call x1, Pallas kernels, device_step(): pl.pallas_call(functools.partial(kernel, group), out_shape=jax.ShapeDtype...  105 us
    unnamed x3, local copies, waits for them, and re-layouts  5.01 us

profile of v1, /device:TPU:21, one launch (start us, length us, event | category | flops | bytes accessed | tf_op | source)
XLA Modules:
  0.0 110.3 jit_solution(10497374531942187564)
XLA Ops:
  0.0 1.4 %copy.11.asg_ref = s32[64,6]{1,0:T(8,128)} copy(s32[64,6]{0,1:T(8,128)} %param.15) | data formatting | bytes 3072 | tf_op args[5]
  1.4 1.9 %copy.12.wr_ref = bf16[2048,64]{1,0:T(8,128)(2,1)} copy(bf16[2048,64]{0,1:T(8,128)(2,1)} %param.16) | data formatting | bytes 524288 | tf_op args[6]
  3.3 105.2 %moe_step.1 = bf16[64,2048]{1,0:T(8,128)(2,1)} custom-call(bf16[64,2048]{1,0:T(8,128)(2,1)} %x_ref.1, s32[64,6]{1,0:T(8,128)} %copy.11.asg_ref, s32[1,80]{1,0:T(1,128)} %bitcast.1, bf16[2048,64]{1,0:T(8,128)(2,1)} %copy.12.wr_ref, bf16[5,2048,1408]{2,1,0:T(8,128)(2,1)} %w1.1, bf16[5,2048,1408]{2,1,0:T(8,128)(2,1)} %w3.1, bf16[5,1408,2048]{2,1,0:T(8,128)(2,1)} %w2.1, ...), custom_call_target="tpu_custom_call" | custom-call | tf_op jit(solution)/shard_map/moe_step/pallas_call | solution.py:432
  108.6 1.7 %copy.14 = bf16[64,2048]{1,0:T(8,128)(2,1)} copy(bf16[64,2048]{1,0:T(8,128)(2,1)} %moe_step.1) | data formatting | bytes 524288

commit v2 on v0

v2 whole, which is shorter than its diff:
```python
import functools

import jax
import jax.numpy as jnp
from jax import lax
from jax.experimental import pallas as pl
from jax.experimental.pallas import tpu as pltpu
from jax.sharding import PartitionSpec as P

ROUTE_SCALE = 2.5
MESH = pl.DeviceIdType.MESH
LANES = 128
CAP = 16
PARTS = 3
K_BLOCKS = 4
A_RING = 18
B_RING = 5
SUB = 256
CHUNKS = 4
EARLY = 2

F32 = jnp.float32
BF16 = jnp.bfloat16


def widths_of(ff):
    wide = -(-(ff // LANES) // PARTS) * LANES
    return wide, [min(wide, ff - t * wide) for t in range(PARTS)]


def kernel(
    group, x_hbm, asg_ref, se_ref, wr_ref, w1, w3, w2, v1, v3, v2, y_hbm,
    xall, tall, tsend, xg, h, ob, osib, s1, r1, sn, rn, yacc, yst, hs, wcs,
    abuf, bbuf,
    xs_sem, xr_sem, xds_sem, xdr_sem, ts_sem, tr_sem, tds_sem, tdr_sem,
    os_sem, or_sem, rs_sem, rr_sem, a_sem, b_sem, x_sem, y_sem,
):
    tok, dim = x_hbm.shape
    top_k = asg_ref.shape[0]
    slots, _, ff = w1.shape
    ff_sh = v1.shape[1]
    nz = group // 2
    far = nz // 2
    cw = dim // CHUNKS
    hw = cw // 2
    piece = tok // 2
    early = 2 * far - 3
    wide, widths = widths_of(ff)
    seg = slots * CAP
    rows_k = dim // K_BLOCKS
    per_slot = 2 * K_BLOCKS
    sh_pieces = ff_sh // ff
    nsb = CHUNKS * slots
    last_b = CHUNKS * (slots + sh_pieces)

    me = lax.axis_index("ep")
    z = me // 2
    c = me % 2
    sib = 2 * z + (1 - c)

    def at(zz):
        return lax.rem(zz + 2 * nz, nz)

    nb = (2 * at(z + 1) + c, 2 * at(z - 1) + c)

    def away(d, s):
        return at(z - s) if d == 0 else at(z + s)

    order = [(0, 0)] + [(d, s) for s in range(1, far) for d in (0, 1)] + [(0, far)]

    def chip(r):
        return away(*order[r])

    def remote(src, dst, ssem, rsem, dev):
        return pltpu.make_async_remote_copy(
            src_ref=src, dst_ref=dst, send_sem=ssem, recv_sem=rsem, device_id={"ep": dev}, device_id_type=MESH
        )

    def a_place(p, j):
        return lax.rem(per_slot * p + j, A_RING)

    def a_copy(p, j):
        rows = pl.ds(j // 2 * rows_k, rows_k)
        if isinstance(p, int) and p < sh_pieces:
            src = (v1, v3)[j % 2].at[rows, pl.ds(p * ff, ff)]
        else:
            src = (w1, w3)[j % 2].at[p - sh_pieces, rows, :]
        return pltpu.make_async_copy(src, abuf.at[a_place(p, j)], a_sem.at[a_place(p, j)])

    def a_wait(p):
        for j in range(per_slot):
            a_copy(p, j).wait()

    def a_ahead(p):
        for j in range(per_slot):
            nxt, to = (j + A_RING) % per_slot, p + (j + A_RING) // per_slot
            pl.when(to < sh_pieces + slots)(lambda: a_copy(to, nxt).start())

    def b_copy(i):
        l = i % slots
        cols = pl.ds(pl.multiple_of(i // slots * cw, LANES), cw)
        slot = i % B_RING
        return pltpu.make_async_copy(w2.at[l, :, cols], bbuf.at[slot], b_sem.at[slot])

    def b_shared(v):
        q, p = v // sh_pieces, v % sh_pieces
        slot = (nsb + v) % B_RING
        return pltpu.make_async_copy(v2.at[pl.ds(p * ff, ff), pl.ds(q * cw, cw)], bbuf.at[slot], b_sem.at[slot])

    def b_first(v):
        return b_copy(v) if v < nsb else b_shared(v - nsb)

    x_own = pltpu.make_async_copy(x_hbm, xall.at[c, z], x_sem)
    x_own.start()

    barrier = pltpu.get_barrier_semaphore()
    for peer in (nb[0], nb[1], sib):
        pl.semaphore_signal(barrier, inc=1, device_id={"ep": peer}, device_id_type=MESH)

    x_own.wait()
    for n in range(per_slot):
        a_copy(0, n).start()
    x_mine = xall[c, z]

    def gates():
        num_slots = se_ref.shape[1]
        num_exp = wr_ref.shape[0]
        exp_ids = lax.broadcasted_iota(jnp.int32, (LANES, LANES), 0)
        slot_lane = jnp.concatenate([se_ref[...], jnp.full((1, LANES - num_slots), -1, jnp.int32)], axis=1)
        holds = jnp.transpose(jnp.where(exp_ids == slot_lane, 1.0, 0.0))[:, :num_exp].astype(BF16)
        w_slot = jnp.dot(holds, wr_ref[...], preferred_element_type=F32).astype(BF16)
        gate = jax.nn.sigmoid(
            lax.dot_general(w_slot, x_mine, (((1,), (1,)), ((), ())), preferred_element_type=F32)
        )
        slot_ids = lax.broadcasted_iota(jnp.int32, (LANES, tok), 0)
        picked = [
            jnp.sum(jnp.where(slot_ids == asg_ref[k : k + 1, :], gate, 0.0), axis=0, keepdims=True)
            for k in range(top_k)
        ]
        total = functools.reduce(lambda a, b: a + b, picked)
        tsend[...] = jnp.full((16, LANES), -1.0, F32)
        for k in range(top_k):
            tsend[k : k + 1, :tok] = asg_ref[k : k + 1, :].astype(F32)
            tsend[8 + k : 9 + k, :tok] = ROUTE_SCALE * picked[k] / jnp.maximum(total, 1e-30)
        tall[c, z] = tsend[...]

    gates()
    pl.semaphore_wait(barrier, 3)

    def start_weights():
        for n in range(per_slot, A_RING):
            a_copy(n // per_slot, n % per_slot).start()
        for v in range(B_RING):
            b_first(v).start()


    def x_rows(d, m):
        return pl.ds(((m % 2) ^ d) * piece, piece)

    def x_send(d, m):
        ref = xall.at[c, away(d, m // 2), x_rows(d, m)]
        return remote(ref, ref, xs_sem.at[d, m], xr_sem.at[d, m], nb[d])

    def x_recv(d, m):
        ref = xall.at[c, away(d, m // 2 + 1), x_rows(d, m)]
        return remote(ref, ref, xs_sem.at[d, m], xr_sem.at[d, m], nb[d])

    def x_cross(d, m, core):
        ref = xall.at[core, away(d, m // 2 + 1), x_rows(d, m)]
        return remote(ref, ref, xds_sem.at[d, m], xdr_sem.at[d, m], sib)

    def x_cross_own(core):
        return remote(xall.at[core, z], xall.at[core, z], xds_sem.at[0, 7], xdr_sem.at[0, 7], sib)

    def t_send(d, m):
        src = tsend if m == 0 else tall.at[c, away(d, m)]
        return remote(src, tall.at[c, away(d, m)], ts_sem.at[d, m], tr_sem.at[d, m], nb[d])

    def t_recv(d, m):
        ref = tall.at[c, away(d, m + 1)]
        return remote(ref, ref, ts_sem.at[d, m], tr_sem.at[d, m], nb[d])

    def t_cross(d, m, core):
        ref = tall.at[core, away(d, m + 1)]
        return remote(ref, ref, tds_sem.at[d, m], tdr_sem.at[d, m], sib)

    def t_cross_own(core):
        return remote(tsend, tall.at[core, z], tds_sem.at[1, far - 1], tdr_sem.at[1, far - 1], sib)

    t_last = (far - 1, far - 2)
    x_last = 2 * far - 2

    def first_x():
        for m in (0, 1):
            for d in (0, 1):
                x_send(d, m).start()
                if m == 0:
                    t_send(d, 0).start()

    def take_x(m):
        for d in (0, 1):
            x_recv(d, m).wait_recv()
            if m + 2 <= x_last:
                x_send(d, m + 2).start()
            x_cross(d, m, c).start()

    def take_t(m):
        for d in (0, 1):
            if m <= t_last[d]:
                t_recv(d, m).wait_recv()
                if m + 1 <= t_last[d]:
                    t_send(d, m + 1).start()
                t_cross(d, m, c).start()

    tri = jnp.where(
        lax.broadcasted_iota(jnp.int32, (LANES, LANES), 0) < lax.broadcasted_iota(jnp.int32, (LANES, LANES), 1), 1.0, 0.0
    ).astype(BF16)

    def choose(tab, rows, slot_of):
        row = lax.broadcasted_iota(jnp.int32, (rows, LANES), 0)
        want = slot_of(row // CAP).astype(F32)
        named = jnp.zeros((rows, LANES), F32)
        weight = jnp.zeros((rows, LANES), F32)
        for k in range(top_k):
            hit = tab[k : k + 1, :] == want
            named = jnp.where(hit, 1.0, named)
            weight = jnp.where(hit, tab[8 + k : 9 + k, :], weight)
        rank = jnp.dot(named.astype(BF16), tri, preferred_element_type=F32)
        return (named > 0.0) & (rank == (row % CAP).astype(F32)), weight

    def dispatch(r, core):
        mine, _ = choose(tall[core, chip(r)], seg, lambda i: me * slots + i)
        pick = jnp.where(mine, 1.0, 0.0).astype(BF16)[:, :tok]
        rows = jnp.dot(pick, xall[core, chip(r)], preferred_element_type=F32).astype(BF16)
        for l in range(slots):
            xg[l, r, core] = rows[l * CAP : (l + 1) * CAP]

    def weigh(r):
        mine, weight = choose(
            tall[c, chip(r)], 2 * seg, lambda i: jnp.where(i < slots, me * slots + i, sib * slots + i - slots)
        )
        full = jnp.where(mine, weight, 0.0)
        full = jnp.concatenate([full, jnp.zeros((2 * LANES - 2 * seg, LANES), F32)], axis=0)
        full = jnp.transpose(full)[:tok]
        hi = full.astype(BF16)
        rest = full - hi.astype(F32)
        mid = rest.astype(BF16)
        low = (rest - mid.astype(F32)).astype(BF16)
        wcs[r] = jnp.concatenate([hi, mid, low], axis=0)

    def spots(s):
        return [r for r, (_, dist) in enumerate(order) if dist == s]

    def ready(s):
        if s == 0:
            t_cross_own(1 - c).wait_recv()
        else:
            for d in (0, 1):
                x_cross(d, 2 * s - 2, 1 - c).wait_recv()
                if s < far:
                    x_cross(d, 2 * s - 1, 1 - c).wait_recv()
                if s - 1 <= t_last[d]:
                    t_cross(d, s - 1, 1 - c).wait_recv()
        for r in spots(s):
            for core in (0, 1):
                dispatch(r, core)

    def weights_of(s):
        for r in spots(s):
            weigh(r)

    def gated(rows, p, t, put):
        end = t * wide + widths[t]
        for off in range(t * wide, end, SUB):
            width = min(SUB, end - off)
            cols = slice(off, off + width)

            def weight(w):
                return jnp.concatenate([abuf[a_place(p, 2 * kb + w), :, cols] for kb in range(K_BLOCKS)], axis=0)

            both = jnp.concatenate([weight(0), weight(1)], axis=1)
            res = jnp.dot(rows, both, preferred_element_type=F32)
            put(off, width, (jax.nn.silu(res[:, :width]) * res[:, width:]).astype(BF16))

    def shared_up(n):
        p, t = n // PARTS, n % PARTS
        if t == 0:
            a_wait(p)

        def put(off, width, val):
            hs[:, p * ff + off : p * ff + off + width] = val

        gated(x_mine, p, t, put)
        if t == PARTS - 1:
            for j in range(per_slot):
                a_copy(p + (j + A_RING) // per_slot, (j + A_RING) % per_slot).start()

    def shared_down(q):
        acc = None
        for p in range(sh_pieces):
            v = q * sh_pieces + p
            b_shared(v).wait()
            part = jnp.dot(hs[:, p * ff : (p + 1) * ff], bbuf[(nsb + v) % B_RING], preferred_element_type=F32)
            acc = part if acc is None else acc + part
            if nsb + v + B_RING < last_b:
                b_first(nsb + v + B_RING).start()
        yacc[q] = yacc[q] + acc

    def up_rows(l, first, last):
        rows = xg[l, first:last].reshape(2 * (last - first) * CAP, dim)
        lo, hi = 2 * first * CAP, 2 * last * CAP

        def put(off, width, val):
            h[l, lo:hi, off : off + width] = val

        for t in range(PARTS):
            gated(rows, l + sh_pieces, t, put)

    def up_near(l):
        a_wait(l + sh_pieces)
        up_rows(l, 0, early)

    def up_far():
        def one(l, _):
            up_rows(l, early, nz)
            a_ahead(l + sh_pieces)
            return 0

        lax.fori_loop(0, EARLY, one, 0)

    def up_all():
        def one(l, _):
            a_wait(l + sh_pieces)
            up_rows(l, 0, nz)
            a_ahead(l + sh_pieces)
            return 0

        lax.fori_loop(EARLY, slots, one, 0)

    def o_cross(q):
        return remote(ob.at[q % 2, :, :, 1 - c], osib.at[q], os_sem.at[q], or_sem.at[q], sib)

    def down(q, hooks):
        if q >= 2:
            o_cross(q - 2).wait_send()

        def one(l, _):
            i = q * slots + l
            b_copy(i).wait()
            res = jnp.dot(h[l], bbuf[i % B_RING], preferred_element_type=F32).astype(BF16)
            ob[q % 2, l] = res.reshape(nz, 2, CAP, cw)

            @pl.when(i + B_RING < nsb)
            def _():
                b_copy(i + B_RING).start()

            for hl, fn in hooks.items():
                pl.when(l == hl)(fn)
            return 0

        lax.fori_loop(0, slots, one, 0)
        o_cross(q).start()
        if q == CHUNKS - 1:
            for v in range(B_RING):
                b_first(nsb + v).start()

    def r_copy(d, k, s):
        src, dst = (s1.at[d, k], r1.at[d, k]) if s == 1 else (sn.at[d, k, s - 2], rn.at[d, k, s - 2])
        return remote(src, dst, rs_sem.at[d, k, s - 1], rr_sem.at[d, k, s - 1], nb[d])

    def partial(k, r):
        rhs = jnp.concatenate([ob[k % 2, :, r, c].reshape(seg, cw), osib[k, :, r].reshape(seg, cw)], axis=0)
        res = jnp.dot(wcs[r][:, : 2 * seg], rhs, preferred_element_type=F32)
        return res[:tok] + res[tok : 2 * tok] + res[2 * tok :]

    def partials(k):
        o_cross(k).wait_recv()
        part = partial(k, nz - 1)
        s1[0, k] = part[:, :hw]
        s1[1, k] = part[:, hw:]
        for s in range(2, far + 1):
            for d in (0, 1):
                sn[d, k, s - 2] = partial(k, order.index((1 - d, far + 1 - s)))
            if s == 2:
                for d in (0, 1):
                    r_copy(d, k, 1).start()
        yacc[k] = partial(k, 0)

    def step(k, s):
        for d in (0, 1):
            r_copy(d, k, s - 1).wait_recv()
            if s == 2:
                cols = slice(0, hw) if d == 0 else slice(hw, cw)
                sn[d, k, 0, :, cols] = sn[d, k, 0, :, cols] + r1[d, k]
            else:
                sn[d, k, s - 2] = sn[d, k, s - 2] + rn[d, k, s - 3]
            r_copy(d, k, s).start()

    def y_out(q):
        return pltpu.make_async_copy(yst.at[q], y_hbm.at[:, pl.ds(q * cw, cw)], y_sem.at[q])

    def finish(k):
        for d in (0, 1):
            r_copy(d, k, far).wait_recv()
        yst[k] = (yacc[k] + rn[0, k, far - 2] + rn[1, k, far - 2]).astype(BF16)
        y_out(k).start()

    x_cross_own(c).start()
    t_cross_own(c).start()
    first_x()
    start_weights()
    shared_up(0)
    take_x(0)
    take_t(0)
    shared_up(1)
    shared_up(2)
    x_cross_own(1 - c).wait_recv()
    ready(0)
    take_x(1)
    weights_of(0)
    shared_up(3)
    take_x(2)
    take_t(1)
    shared_up(4)
    shared_up(5)
    ready(1)
    take_x(3)
    weights_of(1)
    take_x(4)
    take_t(2)
    ready(2)
    up_near(0)
    take_x(5)
    take_t(3)
    up_near(1)
    take_x(6)
    weights_of(2)
    ready(3)
    weights_of(3)
    weights_of(4)
    ready(4)
    up_far()
    up_all()
    down(0, {})
    down(1, {1: lambda: partials(0)})
    down(2, {1: lambda: partials(1), 4: lambda: step(0, 2)})
    down(3, {1: lambda: partials(2), 3: lambda: step(1, 2)})
    step(0, 3)
    partials(3)
    step(2, 2)
    step(1, 3)
    step(3, 2)
    shared_down(0)
    step(0, 4)
    shared_down(1)
    step(2, 3)
    shared_down(2)
    step(1, 4)
    shared_down(3)
    step(3, 3)
    finish(0)
    step(2, 4)
    finish(1)
    step(3, 4)
    finish(2)
    finish(3)

    for d in (0, 1):
        for m in range(x_last + 1):
            x_send(d, m).wait_send()
            x_cross(d, m, c).wait_send()
        for m in range(t_last[d] + 1):
            t_send(d, m).wait_send()
            t_cross(d, m, c).wait_send()
        for k in range(CHUNKS):
            for s in range(1, far + 1):
                r_copy(d, k, s).wait_send()
    x_cross_own(c).wait_send()
    t_cross_own(c).wait_send()
    for k in (CHUNKS - 2, CHUNKS - 1):
        o_cross(k).wait_send()
    for q in range(CHUNKS):
        y_out(q).wait()


def solution(mesh):
    group = mesh.shape["ep"]

    def device_step(x, slot_expert, w1, w3, w2, assign, w_router, v1, v3, v2):
        tok, dim = x.shape
        slots, _, ff = w1.shape
        nz = group // 2
        far = nz // 2
        cw = dim // CHUNKS
        vmem = pl.BlockSpec(memory_space=pltpu.VMEM)
        hbm = pl.BlockSpec(memory_space=pl.ANY)
        dma = pltpu.SemaphoreType.DMA
        return pl.pallas_call(
            functools.partial(kernel, group),
            out_shape=jax.ShapeDtypeStruct((tok, dim), BF16),
            in_specs=[hbm] + [vmem] * 3 + [hbm] * 6,
            out_specs=hbm,
            scratch_shapes=[
                pltpu.VMEM((2, nz, tok, dim), BF16),
                pltpu.VMEM((2, nz, 16, LANES), F32),
                pltpu.VMEM((16, LANES), F32),
                pltpu.VMEM((slots, nz, 2, CAP, dim), BF16),
                pltpu.VMEM((slots, nz * 2 * CAP, ff), BF16),
                pltpu.VMEM((2, slots, nz, 2, CAP, cw), BF16),
                pltpu.VMEM((CHUNKS, slots, nz, CAP, cw), BF16),
                pltpu.VMEM((2, CHUNKS, tok, cw // 2), F32),
                pltpu.VMEM((2, CHUNKS, tok, cw // 2), F32),
                pltpu.VMEM((2, CHUNKS, far - 1, tok, cw), F32),
                pltpu.VMEM((2, CHUNKS, far - 1, tok, cw), F32),
                pltpu.VMEM((CHUNKS, tok, cw), F32),
                pltpu.VMEM((CHUNKS, tok, cw), BF16),
                pltpu.VMEM((tok, v1.shape[1]), BF16),
                pltpu.VMEM((nz, 3 * tok, 2 * LANES), BF16),
                pltpu.VMEM((A_RING, dim // K_BLOCKS, ff), BF16),
                pltpu.VMEM((B_RING, ff, cw), BF16),
                dma((2, 8)), dma((2, 8)), dma((2, 8)), dma((2, 8)),
                dma((2, far)), dma((2, far)), dma((2, far)), dma((2, far)),
                dma((CHUNKS,)), dma((CHUNKS,)), dma((2, CHUNKS, far)), dma((2, CHUNKS, far)),
                dma((A_RING,)), dma((B_RING,)), dma(()), dma((CHUNKS,)),
            ],
            compiler_params=pltpu.CompilerParams(
                collective_id=0, has_side_effects=True, vmem_limit_bytes=67_000_000
            ),
            name="moe_step",
        )(x, assign.T, slot_expert.reshape(1, -1), w_router.T, w1, w3, w2, v1, v3, v2)

    token_spec = P(("dp", "ep"), None)
    slot_spec = P("ep", None, None)
    return jax.shard_map(
        device_step,
        mesh=mesh,
        in_specs=(token_spec, P(), slot_spec, slot_spec, slot_spec, token_spec, P(), P(), P(), P()),
        out_specs=token_spec,
        check_vma=False,
    )
```

time: 340 us -> 105 us (0.31)
  blocking collectives: 118 us -> 0 us
  Pallas kernels: 0 us -> 103 us
  waiting for transfers between devices: 91.3 us -> 0 us
  matrix products: 70 us -> 0 us
  local copies, waits for them, and re-layouts: 47.5 us -> 1.67 us
  other arithmetic: 7.52 us -> 0 us
  starting transfers between devices: 5.06 us -> 0 us
    all_to_all x1 -> x0, blocking collectives: 118 us -> none  [device_step(): recv_rows = lax.all_to_all(send_rows, 'ep', 0, 0, tiled=True)]
    pallas_call x0 -> x1, Pallas kernels: none -> 103 us  [device_step(): pl.pallas_call(functools.partial(kernel, group), out_shape=jax.ShapeDtype...]
    all_to_all x1 -> x0, waiting for transfers between devices: 91.3 us -> none  [device_step(): lax.all_to_all(expert_out.reshape(dummy_row, dim_model), 'ep', 0, 0, tile...]
    dot_general x6 -> x0, matrix products: 70 us -> none  [the longest x1 21.2 us: device_step(): jnp.einsum('jlcd,ldf->jlcf', recv_rows, w1_slots, preferred_element_type=...]
    gather x9 -> x0, local copies, waits for them, and re-layouts: 27.7 us -> none  [the longest x2 11.3 us: device_step(): send_rows = jnp.take(x_tokens, row_token, axis=0, mode='fill', fill_value=0)]
    all_to_all x3 -> x0, local copies, waits for them, and re-layouts: 14.8 us -> none  [the longest x2 10.1 us: device_step(): lax.all_to_all(expert_out.reshape(dummy_row, dim_model), 'ep', 0, 0, tile...]
    all_to_all x1 -> x0, starting transfers between devices: 5.06 us -> none  [device_step(): lax.all_to_all(expert_out.reshape(dummy_row, dim_model), 'ep', 0, 0, tile...]
    reduce_sum x3 -> x0, other arithmetic: 3.56 us -> none  [the longest x1 3.32 us: device_step(): routed = jnp.sum(route_weight[:, :, None] * gathered, axis=1)]
  transfers between devices with their start and end apart: 1 -> 0, of which waited for: 1 -> 0; matrix products, arithmetic and copies ran while one was open for 4% -> 0% of each run, Pallas kernels for 0% -> 0%
where the time goes in v2:
time: 105 us
  Pallas kernels  103 us (98%)
  local copies, waits for them, and re-layouts  1.67 us (2%)
    pallas_call x1, Pallas kernels, device_step(): pl.pallas_call(functools.partial(kernel, group), out_shape=jax.ShapeDtype...  103 us

profile of v2, /device:TPU:21, one launch (start us, length us, event | category | flops | bytes accessed | tf_op | source)
XLA Modules:
  0.0 105.1 jit_solution(14378692046757116426)
XLA Ops:
  0.0 103.5 %moe_step.1 = bf16[64,2048]{1,0:T(8,128)(2,1)} custom-call(bf16[64,2048]{1,0:T(8,128)(2,1)} %x_hbm.1, s32[6,64]{1,0:T(8,128)} %bitcast.4, s32[1,80]{1,0:T(1,128)} %bitcast.5, bf16[64,2048]{1,0:T(8,128)(2,1)} %bitcast.3, bf16[5,2048,1408]{2,1,0:T(8,128)(2,1)} %w1.1, bf16[5,2048,1408]{2,1,0:T(8,128)(2,1)} %w3.1, bf16[5,1408,2048]{2,1,0:T(8,128)(2,1)} %w2.1, ...), custom_call_target="tpu_custom_call" | custom-call | tf_op jit(solution)/shard_map/moe_step/pallas_call | solution.py:498
  103.5 1.7 %copy.12 = bf16[64,2048]{1,0:T(8,128)(2,1)} copy(bf16[64,2048]{1,0:T(8,128)(2,1)} %moe_step.1) | data formatting | bytes 524288

commit v3 on v2

--- a/solution.py
+++ b/solution.py
@@ -15,8 +15,9 @@
 K_BLOCKS = 4
 A_RING = 18
 B_RING = 5
-SUB = 256
+SUB = 512
 CHUNKS = 4
+UNITS = 2 * CHUNKS
 EARLY = 2
 
 F32 = jnp.float32
@@ -29,20 +30,21 @@
 
 
 def kernel(
-    group, x_hbm, asg_ref, se_ref, wr_ref, w1, w3, w2, v1, v3, v2, y_hbm,
-    xall, tall, tsend, xg, h, ob, osib, s1, r1, sn, rn, yacc, yst, hs, wcs,
+    group, x_hbm, asg_hbm, se_hbm, wr_hbm, w1, w3, w2, v1, v3, v2, y_hbm,
+    asg_ref, se_ref, wr_ref, xall, tall, tsend, xg, h, ob, osib, s1, r1, sn, rn, yacc, yst, hs, wcs,
     abuf, bbuf,
     xs_sem, xr_sem, xds_sem, xdr_sem, ts_sem, tr_sem, tds_sem, tdr_sem,
-    os_sem, or_sem, rs_sem, rr_sem, a_sem, b_sem, x_sem, y_sem,
+    os_sem, or_sem, rs_sem, rr_sem, a_sem, b_sem, x_sem, g_sem, y_sem,
 ):
     tok, dim = x_hbm.shape
-    top_k = asg_ref.shape[0]
+    top_k = asg_hbm.shape[0]
     slots, _, ff = w1.shape
     ff_sh = v1.shape[1]
     nz = group // 2
     far = nz // 2
     cw = dim // CHUNKS
-    hw = cw // 2
+    uw = dim // UNITS
+    hw = uw // 2
     piece = tok // 2
     early = 2 * far - 3
     wide, widths = widths_of(ff)
@@ -112,6 +114,12 @@
 
     x_own = pltpu.make_async_copy(x_hbm, xall.at[c, z], x_sem)
     x_own.start()
+    gate_copies = [
+        pltpu.make_async_copy(src, dst, g_sem.at[i])
+        for i, (src, dst) in enumerate(((asg_hbm, asg_ref), (se_hbm, se_ref), (wr_hbm, wr_ref)))
+    ]
+    for cp in gate_copies:
+        cp.start()
 
     barrier = pltpu.get_barrier_semaphore()
     for peer in (nb[0], nb[1], sib):
@@ -123,6 +131,8 @@
     x_mine = xall[c, z]
 
     def gates():
+        for cp in gate_copies:
+            cp.wait()
         num_slots = se_ref.shape[1]
         num_exp = wr_ref.shape[0]
         exp_ids = lax.broadcasted_iota(jnp.int32, (LANES, LANES), 0)
@@ -144,7 +154,6 @@
             tsend[8 + k : 9 + k, :tok] = ROUTE_SCALE * picked[k] / jnp.maximum(total, 1e-30)
         tall[c, z] = tsend[...]
 
-    gates()
     pl.semaphore_wait(barrier, 3)
 
     def start_weights():
@@ -190,12 +199,9 @@
     t_last = (far - 1, far - 2)
     x_last = 2 * far - 2
 
-    def first_x():
-        for m in (0, 1):
-            for d in (0, 1):
-                x_send(d, m).start()
-                if m == 0:
-                    t_send(d, 0).start()
+    def first_x(m):
+        for d in (0, 1):
+            x_send(d, m).start()
 
     def take_x(m):
         for d in (0, 1):
@@ -228,12 +234,21 @@
         rank = jnp.dot(named.astype(BF16), tri, preferred_element_type=F32)
         return (named > 0.0) & (rank == (row % CAP).astype(F32)), weight
 
-    def dispatch(r, core):
-        mine, _ = choose(tall[core, chip(r)], seg, lambda i: me * slots + i)
-        pick = jnp.where(mine, 1.0, 0.0).astype(BF16)[:, :tok]
-        rows = jnp.dot(pick, xall[core, chip(r)], preferred_element_type=F32).astype(BF16)
-        for l in range(slots):
-            xg[l, r, core] = rows[l * CAP : (l + 1) * CAP]
+    def dispatch(blocks):
+        picks = []
+        for r, core in blocks:
+            mine, _ = choose(tall[core, chip(r)], seg, lambda i: me * slots + i)
+            picks.append(jnp.where(mine, 1.0, 0.0).astype(BF16)[:, :tok])
+
+        def one(i, _):
+            cols = pl.ds(pl.multiple_of(i * cw, LANES), cw)
+            for (r, core), pick in zip(blocks, picks):
+                rows = jnp.dot(pick, xall[core, chip(r), :, cols], preferred_element_type=F32).astype(BF16)
+                for l in range(slots):
+                    xg[l, r, core, :, cols] = rows[l * CAP : (l + 1) * CAP]
+            return 0
+
+        lax.fori_loop(0, CHUNKS, one, 0)
 
     def weigh(r):
         mine, weight = choose(
@@ -261,9 +276,7 @@
                     x_cross(d, 2 * s - 1, 1 - c).wait_recv()
                 if s - 1 <= t_last[d]:
                     t_cross(d, s - 1, 1 - c).wait_recv()
-        for r in spots(s):
-            for core in (0, 1):
-                dispatch(r, core)
+        dispatch([(r, core) for r in spots(s) for core in (0, 1)])
 
     def weights_of(s):
         for r in spots(s):
@@ -337,18 +350,20 @@
 
         lax.fori_loop(EARLY, slots, one, 0)
 
-    def o_cross(q):
-        return remote(ob.at[q % 2, :, :, 1 - c], osib.at[q], os_sem.at[q], or_sem.at[q], sib)
+    def o_cross(q, l):
+        return remote(ob.at[q % 2, l, :, 1 - c], osib.at[q, l], os_sem.at[q, l], or_sem.at[q, l], sib)
 
     def down(q, hooks):
         if q >= 2:
-            o_cross(q - 2).wait_send()
+            for l in range(slots):
+                o_cross(q - 2, l).wait_send()
 
         def one(l, _):
             i = q * slots + l
             b_copy(i).wait()
             res = jnp.dot(h[l], bbuf[i % B_RING], preferred_element_type=F32).astype(BF16)
             ob[q % 2, l] = res.reshape(nz, 2, CAP, cw)
+            o_cross(q, l).start()
 
             @pl.when(i + B_RING < nsb)
             def _():
@@ -359,7 +374,6 @@
             return 0
 
         lax.fori_loop(0, slots, one, 0)
-        o_cross(q).start()
         if q == CHUNKS - 1:
             for v in range(B_RING):
                 b_first(nsb + v).start()
@@ -374,96 +388,114 @@
         return res[:tok] + res[tok : 2 * tok] + res[2 * tok :]
 
     def partials(k):
-        o_cross(k).wait_recv()
+        for l in range(slots):
+            o_cross(k, l).wait_recv()
         part = partial(k, nz - 1)
-        s1[0, k] = part[:, :hw]
-        s1[1, k] = part[:, hw:]
+        for u in (0, 1):
+            s1[0, 2 * k + u] = part[:, u * uw : u * uw + hw]
+            s1[1, 2 * k + u] = part[:, u * uw + hw : (u + 1) * uw]
         for s in range(2, far + 1):
             for d in (0, 1):
-                sn[d, k, s - 2] = partial(k, order.index((1 - d, far + 1 - s)))
+                part = partial(k, order.index((1 - d, far + 1 - s)))
+                for u in (0, 1):
+                    sn[d, 2 * k + u, s - 2] = part[:, u * uw : (u + 1) * uw]
             if s == 2:
-                for d in (0, 1):
-                    r_copy(d, k, 1).start()
+                for u in (0, 1):
+                    for d in (0, 1):
+                        r_copy(d, 2 * k + u, 1).start()
         yacc[k] = partial(k, 0)
 
-    def step(k, s):
+    def step(u, s):
         for d in (0, 1):
-            r_copy(d, k, s - 1).wait_recv()
+            r_copy(d, u, s - 1).wait_recv()
             if s == 2:
-                cols = slice(0, hw) if d == 0 else slice(hw, cw)
-                sn[d, k, 0, :, cols] = sn[d, k, 0, :, cols] + r1[d, k]
+                cols = slice(0, hw) if d == 0 else slice(hw, uw)
+                sn[d, u, 0, :, cols] = sn[d, u, 0, :, cols] + r1[d, u]
             else:
-                sn[d, k, s - 2] = sn[d, k, s - 2] + rn[d, k, s - 3]
-            r_copy(d, k, s).start()
-
-    def y_out(q):
-        return pltpu.make_async_copy(yst.at[q], y_hbm.at[:, pl.ds(q * cw, cw)], y_sem.at[q])
-
-    def finish(k):
+                sn[d, u, s - 2] = sn[d, u, s - 2] + rn[d, u, s - 3]
+            r_copy(d, u, s).start()
+
+    def y_out(u):
+        return pltpu.make_async_copy(yst.at[u], y_hbm.at[:, pl.ds(u * uw, uw)], y_sem.at[u])
+
+    def finish(u):
+        mine = yacc[u // 2, :, u % 2 * uw : (u % 2 + 1) * uw]
         for d in (0, 1):
-            r_copy(d, k, far).wait_recv()
-        yst[k] = (yacc[k] + rn[0, k, far - 2] + rn[1, k, far - 2]).astype(BF16)
-        y_out(k).start()
+            r_copy(d, u, far).wait_recv()
+        yst[u] = (mine + rn[0, u, far - 2] + rn[1, u, far - 2]).astype(BF16)
+        y_out(u).start()
 
     x_cross_own(c).start()
+    first_x(0)
+    gates()
+    for d in (0, 1):
+        t_send(d, 0).start()
     t_cross_own(c).start()
-    first_x()
+    first_x(1)
     start_weights()
     shared_up(0)
     take_x(0)
     take_t(0)
     shared_up(1)
     shared_up(2)
+    take_x(1)
     x_cross_own(1 - c).wait_recv()
     ready(0)
-    take_x(1)
     weights_of(0)
     shared_up(3)
     take_x(2)
     take_t(1)
     shared_up(4)
     shared_up(5)
+    take_x(3)
     ready(1)
-    take_x(3)
     weights_of(1)
+    weights_of(2)
     take_x(4)
     take_t(2)
     ready(2)
     up_near(0)
     take_x(5)
+    up_near(1)
+    weights_of(3)
+    take_x(6)
     take_t(3)
-    up_near(1)
-    take_x(6)
-    weights_of(2)
     ready(3)
-    weights_of(3)
     weights_of(4)
     ready(4)
     up_far()
     up_all()
     down(0, {})
     down(1, {1: lambda: partials(0)})
-    down(2, {1: lambda: partials(1), 4: lambda: step(0, 2)})
-    down(3, {1: lambda: partials(2), 3: lambda: step(1, 2)})
-    step(0, 3)
+    down(2, {0: lambda: partials(1), 1: lambda: step(0, 2), 2: lambda: step(1, 2)})
+    down(3, {0: lambda: [step(2, 2), step(3, 2), partials(2)] and None, 1: lambda: step(0, 3), 2: lambda: step(1, 3)})
     partials(3)
-    step(2, 2)
-    step(1, 3)
-    step(3, 2)
+    step(4, 2)
+    step(5, 2)
+    step(2, 3)
+    step(3, 3)
+    step(0, 4)
+    step(1, 4)
+    step(6, 2)
+    step(7, 2)
     shared_down(0)
-    step(0, 4)
+    step(4, 3)
+    step(5, 3)
     shared_down(1)
-    step(2, 3)
+    step(2, 4)
+    step(3, 4)
     shared_down(2)
-    step(1, 4)
+    step(6, 3)
+    step(7, 3)
     shared_down(3)
-    step(3, 3)
+    step(4, 4)
+    step(5, 4)
     finish(0)
-    step(2, 4)
     finish(1)
-    step(3, 4)
-    finish(2)
-    finish(3)
+    step(6, 4)
+    step(7, 4)
+    for u in range(2, UNITS):
+        finish(u)
 
     for d in (0, 1):
         for m in range(x_last + 1):
@@ -472,15 +504,16 @@
         for m in range(t_last[d] + 1):
             t_send(d, m).wait_send()
             t_cross(d, m, c).wait_send()
-        for k in range(CHUNKS):
+        for k in range(UNITS):
             for s in range(1, far + 1):
                 r_copy(d, k, s).wait_send()
     x_cross_own(c).wait_send()
     t_cross_own(c).wait_send()
     for k in (CHUNKS - 2, CHUNKS - 1):
-        o_cross(k).wait_send()
-    for q in range(CHUNKS):
-        y_out(q).wait()
+        for l in range(slots):
+            o_cross(k, l).wait_send()
+    for u in range(UNITS):
+        y_out(u).wait()
 
 
 def solution(mesh):
@@ -491,16 +524,18 @@
         slots, _, ff = w1.shape
         nz = group // 2
         far = nz // 2
-        cw = dim // CHUNKS
-        vmem = pl.BlockSpec(memory_space=pltpu.VMEM)
+        cw, uw = dim // CHUNKS, dim // UNITS
         hbm = pl.BlockSpec(memory_space=pl.ANY)
         dma = pltpu.SemaphoreType.DMA
         return pl.pallas_call(
             functools.partial(kernel, group),
             out_shape=jax.ShapeDtypeStruct((tok, dim), BF16),
-            in_specs=[hbm] + [vmem] * 3 + [hbm] * 6,
+            in_specs=[hbm] * 10,
             out_specs=hbm,
             scratch_shapes=[
+                pltpu.VMEM((assign.shape[1], tok), jnp.int32),
+                pltpu.VMEM((1, slot_expert.shape[0]), jnp.int32),
+                pltpu.VMEM((w_router.shape[1], dim), BF16),
                 pltpu.VMEM((2, nz, tok, dim), BF16),
                 pltpu.VMEM((2, nz, 16, LANES), F32),
                 pltpu.VMEM((16, LANES), F32),
@@ -508,20 +543,20 @@
                 pltpu.VMEM((slots, nz * 2 * CAP, ff), BF16),
                 pltpu.VMEM((2, slots, nz, 2, CAP, cw), BF16),
                 pltpu.VMEM((CHUNKS, slots, nz, CAP, cw), BF16),
-                pltpu.VMEM((2, CHUNKS, tok, cw // 2), F32),
-                pltpu.VMEM((2, CHUNKS, tok, cw // 2), F32),
-                pltpu.VMEM((2, CHUNKS, far - 1, tok, cw), F32),
-                pltpu.VMEM((2, CHUNKS, far - 1, tok, cw), F32),
+                pltpu.VMEM((2, UNITS, tok, uw // 2), F32),
+                pltpu.VMEM((2, UNITS, tok, uw // 2), F32),
+                pltpu.VMEM((2, UNITS, far - 1, tok, uw), F32),
+                pltpu.VMEM((2, UNITS, far - 1, tok, uw), F32),
                 pltpu.VMEM((CHUNKS, tok, cw), F32),
-                pltpu.VMEM((CHUNKS, tok, cw), BF16),
+                pltpu.VMEM((UNITS, tok, uw), BF16),
                 pltpu.VMEM((tok, v1.shape[1]), BF16),
                 pltpu.VMEM((nz, 3 * tok, 2 * LANES), BF16),
                 pltpu.VMEM((A_RING, dim // K_BLOCKS, ff), BF16),
                 pltpu.VMEM((B_RING, ff, cw), BF16),
                 dma((2, 8)), dma((2, 8)), dma((2, 8)), dma((2, 8)),
                 dma((2, far)), dma((2, far)), dma((2, far)), dma((2, far)),
-                dma((CHUNKS,)), dma((CHUNKS,)), dma((2, CHUNKS, far)), dma((2, CHUNKS, far)),
-                dma((A_RING,)), dma((B_RING,)), dma(()), dma((CHUNKS,)),
+                dma((CHUNKS, slots)), dma((CHUNKS, slots)), dma((2, UNITS, far)), dma((2, UNITS, far)),
+                dma((A_RING,)), dma((B_RING,)), dma(()), dma((3,)), dma((UNITS,)),
             ],
             compiler_params=pltpu.CompilerParams(
                 collective_id=0, has_side_effects=True, vmem_limit_bytes=67_000_000

time: 105 us -> 103 us (0.981)
  Pallas kernels: 103 us -> 101 us
    pallas_call x1, Pallas kernels: 103 us -> 101 us  [device_step(): pl.pallas_call(functools.partial(kernel, group), out_shape=jax.ShapeDtype...]
where the time goes in v3:
time: 103 us
  Pallas kernels  101 us (98%)
  local copies, waits for them, and re-layouts  1.67 us (2%)
    pallas_call x1, Pallas kernels, device_step(): pl.pallas_call(functools.partial(kernel, group), out_shape=jax.ShapeDtype...  101 us

profile of v3, /device:TPU:21, one launch (start us, length us, event | category | flops | bytes accessed | tf_op | source)
XLA Modules:
  0.0 102.7 jit_solution(9240832862755175574)
XLA Ops:
  0.0 101.0 %moe_step.1 = bf16[64,2048]{1,0:T(8,128)(2,1)} custom-call(bf16[64,2048]{1,0:T(8,128)(2,1)} %x_hbm.1, s32[6,64]{1,0:T(8,128)} %bitcast.4, s32[1,80]{1,0:T(1,128)} %bitcast.5, bf16[64,2048]{1,0:T(8,128)(2,1)} %bitcast.3, bf16[5,2048,1408]{2,1,0:T(8,128)(2,1)} %w1.1, bf16[5,2048,1408]{2,1,0:T(8,128)(2,1)} %w3.1, bf16[5,1408,2048]{2,1,0:T(8,128)(2,1)} %w2.1, ...), custom_call_target="tpu_custom_call" | custom-call | tf_op jit(solution)/shard_map/moe_step/pallas_call | solution.py:530
  101.0 1.7 %copy.12 = bf16[64,2048]{1,0:T(8,128)(2,1)} copy(bf16[64,2048]{1,0:T(8,128)(2,1)} %moe_step.1) | data formatting | bytes 524288

commit v4 on v3

--- a/solution.py
+++ b/solution.py
@@ -358,22 +358,20 @@
             for l in range(slots):
                 o_cross(q - 2, l).wait_send()
 
-        def one(l, _):
-            i = q * slots + l
-            b_copy(i).wait()
-            res = jnp.dot(h[l], bbuf[i % B_RING], preferred_element_type=F32).astype(BF16)
-            ob[q % 2, l] = res.reshape(nz, 2, CAP, cw)
-            o_cross(q, l).start()
-
-            @pl.when(i + B_RING < nsb)
-            def _():
-                b_copy(i + B_RING).start()
-
-            for hl, fn in hooks.items():
-                pl.when(l == hl)(fn)
-            return 0
-
-        lax.fori_loop(0, slots, one, 0)
+        for first in range(0, slots, 2):
+            pair = range(first, min(first + 2, slots))
+            for l in pair:
+                b_copy(q * slots + l).wait()
+            for l in pair:
+                i = q * slots + l
+                res = jnp.dot(h[l], bbuf[i % B_RING], preferred_element_type=F32).astype(BF16)
+                ob[q % 2, l] = res.reshape(nz, 2, CAP, cw)
+            for l in pair:
+                o_cross(q, l).start()
+                if q * slots + l + B_RING < nsb:
+                    b_copy(q * slots + l + B_RING).start()
+            for fn in hooks.get(first, ()):
+                fn()
         if q == CHUNKS - 1:
             for v in range(B_RING):
                 b_first(nsb + v).start()
@@ -457,18 +455,19 @@
     up_near(0)
     take_x(5)
     up_near(1)
-    weights_of(3)
     take_x(6)
     take_t(3)
     ready(3)
-    weights_of(4)
     ready(4)
     up_far()
     up_all()
     down(0, {})
-    down(1, {1: lambda: partials(0)})
-    down(2, {0: lambda: partials(1), 1: lambda: step(0, 2), 2: lambda: step(1, 2)})
-    down(3, {0: lambda: [step(2, 2), step(3, 2), partials(2)] and None, 1: lambda: step(0, 3), 2: lambda: step(1, 3)})
+    weights_of(3)
+    weights_of(4)
+    part = functools.partial
+    down(1, {0: [part(partials, 0)]})
+    down(2, {0: [part(step, 0, 2), part(step, 1, 2), part(partials, 1)]})
+    down(3, {0: [part(step, 2, 2), part(partials, 2)], 2: [part(step, 3, 2), part(step, 0, 3)], 4: [part(step, 1, 3)]})
     partials(3)
     step(4, 2)
     step(5, 2)

time: 103 us -> 101 us (0.981)
  Pallas kernels: 101 us -> 99.4 us
    pallas_call x1, Pallas kernels: 101 us -> 99.4 us  [device_step(): pl.pallas_call(functools.partial(kernel, group), out_shape=jax.ShapeDtype...]
where the time goes in v4:
time: 101 us
  Pallas kernels  99.4 us (98%)
  local copies, waits for them, and re-layouts  1.67 us (2%)
    pallas_call x1, Pallas kernels, device_step(): pl.pallas_call(functools.partial(kernel, group), out_shape=jax.ShapeDtype...  99.4 us

profile of v4, /device:TPU:21, one launch (start us, length us, event | category | flops | bytes accessed | tf_op | source)
XLA Modules:
  0.0 101.1 jit_solution(13648610633906296271)
XLA Ops:
  0.0 99.4 %moe_step.1 = bf16[64,2048]{1,0:T(8,128)(2,1)} custom-call(bf16[64,2048]{1,0:T(8,128)(2,1)} %x_hbm.1, s32[6,64]{1,0:T(8,128)} %bitcast.4, s32[1,80]{1,0:T(1,128)} %bitcast.5, bf16[64,2048]{1,0:T(8,128)(2,1)} %bitcast.3, bf16[5,2048,1408]{2,1,0:T(8,128)(2,1)} %w1.1, bf16[5,2048,1408]{2,1,0:T(8,128)(2,1)} %w3.1, bf16[5,1408,2048]{2,1,0:T(8,128)(2,1)} %w2.1, ...), custom_call_target="tpu_custom_call" | custom-call | tf_op jit(solution)/shard_map/moe_step/pallas_call | solution.py:529
  99.4 1.7 %copy.12 = bf16[64,2048]{1,0:T(8,128)(2,1)} copy(bf16[64,2048]{1,0:T(8,128)(2,1)} %moe_step.1) | data formatting | bytes 524288

commit v5 on v4

--- a/solution.py
+++ b/solution.py
@@ -447,27 +447,27 @@
     shared_up(5)
     take_x(3)
     ready(1)
+    ready(2)
     weights_of(1)
     weights_of(2)
     take_x(4)
     take_t(2)
-    ready(2)
     up_near(0)
     take_x(5)
     up_near(1)
+    ready(3)
     take_x(6)
     take_t(3)
-    ready(3)
+    weights_of(3)
+    weights_of(4)
     ready(4)
     up_far()
     up_all()
     down(0, {})
-    weights_of(3)
-    weights_of(4)
     part = functools.partial
     down(1, {0: [part(partials, 0)]})
-    down(2, {0: [part(step, 0, 2), part(step, 1, 2), part(partials, 1)]})
-    down(3, {0: [part(step, 2, 2), part(partials, 2)], 2: [part(step, 3, 2), part(step, 0, 3)], 4: [part(step, 1, 3)]})
+    down(2, {0: [part(partials, 1)], 2: [part(step, 0, 2), part(step, 1, 2)]})
+    down(3, {0: [part(partials, 2), part(step, 2, 2), part(step, 3, 2)], 2: [part(step, 0, 3)], 4: [part(step, 1, 3)]})
     partials(3)
     step(4, 2)
     step(5, 2)

time: 101 us -> 102 us (level)
  no operation moved by 1% of the time
where the time goes in v5:
time: 102 us
  Pallas kernels  99.9 us (98%)
  local copies, waits for them, and re-layouts  1.67 us (2%)
    pallas_call x1, Pallas kernels, device_step(): pl.pallas_call(functools.partial(kernel, group), out_shape=jax.ShapeDtype...  99.9 us

profile of v5, /device:TPU:21, one launch (start us, length us, event | category | flops | bytes accessed | tf_op | source)
XLA Modules:
  0.0 101.6 jit_solution(13900978867734418456)
XLA Ops:
  0.0 99.9 %moe_step.1 = bf16[64,2048]{1,0:T(8,128)(2,1)} custom-call(bf16[64,2048]{1,0:T(8,128)(2,1)} %x_hbm.1, s32[6,64]{1,0:T(8,128)} %bitcast.4, s32[1,80]{1,0:T(1,128)} %bitcast.5, bf16[64,2048]{1,0:T(8,128)(2,1)} %bitcast.3, bf16[5,2048,1408]{2,1,0:T(8,128)(2,1)} %w1.1, bf16[5,2048,1408]{2,1,0:T(8,128)(2,1)} %w3.1, bf16[5,1408,2048]{2,1,0:T(8,128)(2,1)} %w2.1, ...), custom_call_target="tpu_custom_call" | custom-call | tf_op jit(solution)/shard_map/moe_step/pallas_call | solution.py:529
  99.9 1.7 %copy.12 = bf16[64,2048]{1,0:T(8,128)(2,1)} copy(bf16[64,2048]{1,0:T(8,128)(2,1)} %moe_step.1) | data formatting | bytes 524288
